TPU v7x, 32 devices: a whole 2x2x4 slice. The times are simulated.
32 devices in a mesh: row: 16 (over z, x, core), chan: 2 (over y).
Axes of the slice: x: 2, y: 2, z: 4, core: 2. Of those that a mesh axis runs over, the one named last changes fastest.
Arguments:
- pair_rep: float32 [256, 256, 128], P('row', 'chan'), may hold values from -630 to 630
- residue_mask: int32 [256], replicated, may hold values from 0 to 1, as said below
- norm_gain: float32 [128], replicated, may hold values from 0.5 to 1.5
- norm_shift: float32 [128], replicated, may hold values from -3 to 3
- proj_weight: float32 [128, 512], replicated, may hold values from -4 to 4
- gate_shift: float32 [128], replicated, may hold values from -4 to 4
- bias_weight: float32 [128, 4], replicated, may hold values from -0.5 to 0.5
- out_weight: float32 [128, 128], replicated, may hold values from -0.5 to 0.5
Outputs:
- update: float32 [256, 256, 128], P('row', 'chan')
Inputs may be any that keep to these rules, and one draw needn't show every extreme that they name: `residue_mask`: residue 0 is always valid.
All inputs are finite; a program needn't handle non-finite values.
Results may differ from a plain program's by a relative error of at most 0.012.
Values may be sent and summed in bfloat16 or wider, within the bound.
A program may use at most 64 MiB of HBM per device.

v0:
```python
import math

import jax
import jax.numpy as jnp
from jax import lax
from jax.sharding import PartitionSpec as P

C = 128
HEADS = 4


def normalize(values, norm_gain, norm_shift):
    average = jnp.mean(values, axis=-1, keepdims=True)
    centered = values - average
    variance = jnp.mean(centered * centered, axis=-1, keepdims=True)
    return centered * lax.rsqrt(variance + 1e-05) * norm_gain + norm_shift


def body(
    pair_rep, residue_mask, norm_gain, norm_shift, proj_weight, gate_shift, bias_weight, out_weight
):
    highest = lax.Precision.HIGHEST
    head_dim = C // HEADS
    scaling = 1.0 / math.sqrt(head_dim)
    pair_rows, span, width = pair_rep.shape
    normed = normalize(pair_rep, norm_gain, norm_shift)
    projected = jnp.einsum("rjc,ce->rje", normed, proj_weight, precision=highest)
    query_half = (
        (projected[:, :, :width] * scaling)
        .astype(jnp.bfloat16)
        .reshape(pair_rows, span, HEADS, head_dim)
    )
    key_half = projected[:, :, width : 2 * width].astype(jnp.bfloat16)
    value_half = projected[:, :, 2 * width : 3 * width].astype(jnp.bfloat16)
    gates = projected[:, :, 3 * width :]
    bias_local = jnp.einsum("rjc,ch->hrj", normed, bias_weight, precision=highest)
    bias_cols = lax.all_gather(bias_local, "row", axis=1, tiled=True)
    own_bias = lax.all_to_all(bias_cols, "chan", split_axis=1, concat_axis=2, tiled=True)
    valid_keys = residue_mask > 0
    key_all, value_all = (
        lax.all_gather(key_half, "chan", axis=1, tiled=True),
        lax.all_gather(value_half, "chan", axis=1, tiled=True),
    )

    def one_row(operands):
        queries, key_row, value_row = operands
        key_heads = key_row.reshape(-1, HEADS, head_dim)
        scores = (
            jnp.einsum("jhd,khd->hjk", queries, key_heads, preferred_element_type=jnp.float32)
            + own_bias
        )
        weights = jax.nn.softmax(
            jnp.where(valid_keys[None, None, :], scores, -1000000000.0), axis=-1
        )
        values = value_row.astype(jnp.float32).reshape(-1, HEADS, head_dim)
        return jnp.einsum("hjk,khd->jhd", weights, values, precision=highest)

    attended = lax.map(one_row, (query_half, key_all, value_all)).reshape(pair_rows, span, width)
    gated_rows = jax.nn.sigmoid(gates + gate_shift) * attended
    return jnp.einsum("rjd,dc->rjc", gated_rows, out_weight, precision=highest)


def solution(mesh):
    return jax.shard_map(
        body,
        mesh=mesh,
        in_specs=(P("row", "chan", None), P(), P(), P(), P(), P(), P(), P()),
        out_specs=P("row", "chan", None),
        check_vma=False,
    )
```

profile of v0, /device:TPU:0, one launch (start us, length us, event | category | flops | bytes accessed | tf_op | source)
XLA Modules:
  0.0 117.3 jit_solution(9026340137136260485)
XLA Ops:
  6.5 1.6 %reduce_sum.27 = f32[16,128]{1,0:T(8,128)S(1)} reduce(f32[16,128,128]{2,1,0:T(8,128)} %param.10, f32[]{:T(128)} %constant.8.clone.1), dimensions={2}, to_apply=%region_0.0 | reduce | flops 260096 | bytes 1056772 | tf_op jit(solution)/shard_map/reduce_sum | solution.py:13
  8.2 1.9 %multiply_reduce_fusion = f32[16,128]{1,0:T(8,128)S(1)} fusion(f32[16,128,128]{2,1,0:T(8,128)} %param.10, f32[16,128]{1,0:T(8,128)S(1)} %broadcast_multiply_fusion), kind=kLoop, calls=%fused_computation.24 | loop fusion | flops 784384 | bytes 1064960 | tf_op jit(solution)/shard_map/reduce_sum | solution.py:15
  10.1 6.7 %fusion.34 = (bf16[16,128,512]{2,1,0:T(8,128)(2,1)S(1)}, f32[16,128,512]{2,1,0:T(8,128)}) fusion(f32[128,512]{1,0:T(8,128)S(1)} %copy-done, f32[16,128,128]{2,1,0:T(8,128)} %param.10, f32[128]{0:T(128)} %param.13, f32[128]{0:T(128)} %param.12, f32[16,128]{1,0:T(8,128)S(1)} %add_rsqrt_fusion, f32[16,128]{1,0:T(8,128)S(1)} %broadcast_multiply_fusion), kind=kOutput, calls=%fused_computation.46 | convolution fusion | flops 1612709888 | bytes 7619584 | tf_op jit(solution)/shard_map/rjc,ce->rje/dot_general | solution.py:27
  16.9 1.3 %fusion.33 = (bf16[16,128,128]{2,1,0:T(8,128)(2,1)}, bf16[16,128,128]{2,1,0:T(8,128)(2,1)}) fusion(bf16[16,128,512]{2,1,0:T(8,128)(2,1)S(1)} %get-tuple-element.84), kind=kLoop, calls=%fused_computation.45 | loop fusion | bytes 2097152 | tf_op jit(solution)/shard_map/slice | solution.py:33
  19.0 1.6 %convolution_bitcast_fusion.1 = f32[4,16,128]{2,0,1:T(4,128)S(1)} fusion(f32[16,128,128]{2,1,0:T(8,128)S(1)} %copy-done.1, f32[128]{0:T(128)S(1)} %copy-done.2, f32[128]{0:T(128)S(1)} %copy-done.3, f32[16,128]{1,0:T(8,128)S(1)} %add_rsqrt_fusion, f32[16,128]{1,0:T(8,128)S(1)} %broadcast_multiply_fusion, f32[128,4]{0,1:T(4,128)S(1)} %copy-done.4), kind=kOutput, calls=%fused_computation.14 | convolution fusion | flops 13631488 | bytes 1100800 | tf_op jit(solution)/shard_map/rjc,ch->hrj/dot_general | solution.py:36
  20.6 26.0 %all_gather.11 = f32[4,256,128]{2,0,1:T(4,128)} all-gather(f32[4,16,128]{2,0,1:T(4,128)S(1)} %convolution_bitcast_fusion.1), channel_id=1, replica_groups=mesh['row'=16,'chan'=2] {'row'}, dimensions={1}, use_global_device_ids=true | all-gather | bytes 557056 | tf_op jit(solution)/shard_map/all_gather | solution.py:37
  46.5 3.5 %all-to-all-start = ((f32[4,256,128]{2,0,1:T(4,128)}), f32[4,256,128]{2,0,1:T(4,128)S(1)}, u32[]{:S(2)}, u32[]{:S(2)}) async-start(f32[4,256,128]{2,0,1:T(4,128)} %all_gather.11), calls=%async_computation | async-start | bytes 1048576 | tf_op jit(solution)/shard_map/all_to_all | solution.py:38
  50.0 1.4 %fusion.9 = bf16[16,128,128]{2,1,0:T(8,128)(2,1)S(1)} fusion(f32[16,128,512]{2,1,0:T(8,128)} %get-tuple-element.85), kind=kLoop, calls=%fused_computation.16 | loop fusion | flops 524288 | bytes 1572864 | tf_op jit(solution)/shard_map/convert_element_type | solution.py:30
  51.8 12.5 %all-to-all-done = f32[4,256,128]{2,0,1:T(4,128)S(1)} async-done(((f32[4,256,128]{2,0,1:T(4,128)}), f32[4,256,128]{2,0,1:T(4,128)S(1)}, u32[]{:S(2)}, u32[]{:S(2)}) %all-to-all-start) | async-done | bytes 524320 | tf_op jit(solution)/shard_map/all_to_all | solution.py:38
  65.2 5.1 %all-gather.5.cloned.1.call-done = bf16[16,256,128]{2,1,0:T(8,128)(2,1)} async-done(((bf16[16,128,128]{2,1,0:T(8,128)(2,1)}), bf16[16,256,128]{2,1,0:T(8,128)(2,1)}) %all-gather.5.cloned.1.call-update) | async-done | bytes 1048592 | tf_op jit(solution)/shard_map/all_gather | solution.py:41
  70.3 36.5 %while.10 = (s32[]{:T(128)}, f32[16,128,4,32]{1,3,2,0:T(8,128)S(1)}, bf16[16,256,128]{2,1,0:T(8,128)(2,1)}, pred[256]{0:T(512)(128)(4,1)S(1)}, bf16[16,128,4,32]...) while((s32[]{:T(128)}, ...), condition=%wide.region_5.6_spmd, body=%wide.region_2.5_spmd.sunk | while | flops 59636736 | bytes 2861665 | solution.py:58
  70.3 0.9 constant_dynamic-slice_fusion.3
  72.6 0.9 constant_dynamic-slice_fusion.3
  74.9 0.9 constant_dynamic-slice_fusion.3
  77.1 0.9 constant_dynamic-slice_fusion.3
  79.4 0.9 constant_dynamic-slice_fusion.3
  81.7 0.9 constant_dynamic-slice_fusion.3
  84.0 0.9 constant_dynamic-slice_fusion.3
  86.2 0.9 constant_dynamic-slice_fusion.3
  88.5 0.9 constant_dynamic-slice_fusion.3
  93.1 0.9 constant_dynamic-slice_fusion.3
  97.6 0.9 constant_dynamic-slice_fusion.3
  102.2 0.9 constant_dynamic-slice_fusion.3
  107.1 3.3 %fusion.15 = f32[16,128,128]{2,1,0:T(8,128)} fusion(f32[16,128,128]{2,1,0:T(8,128)S(1)} %copy.23, f32[16,128,512]{2,1,0:T(8,128)} %get-tuple-element.85, f32[128]{0:T(128)S(1)} %copy-done.7, f32[128,128]{1,0:T(8,128)S(1)} %copy-done.5), kind=kOutput, calls=%fused_computation.25 | convolution fusion | flops 403963904 | bytes 3211776 | tf_op jit(solution)/shard_map/rjd,dc->rjc/dot_general | solution.py:60
  (113 shorter events, 27.7 us)
Async XLA Ops:
  6.5 3.5 %copy-start = (f32[128,512]{1,0:T(8,128)S(1)}, f32[128,512]{1,0:T(8,128)}, u32[]{:S(2)}) copy-start(f32[128,512]{1,0:T(8,128)} %param.14) | copy-start | bytes 786436
  6.5 58.7 %all-gather.3.cloned.1.call-start = ((), (), s32[]{:S(2)}) async-start(), calls=%async_computation.1 | async-start | bytes 1572864 | tf_op jit(solution)/shard_map/all_gather | solution.py:42
  10.1 8.9 %copy-start.1 = (f32[16,128,128]{2,1,0:T(8,128)S(1)}, f32[16,128,128]{2,1,0:T(8,128)}, u32[]{:S(2)}) copy-start(f32[16,128,128]{2,1,0:T(8,128)} %param.10) | copy-start | bytes 3145732
  10.1 8.9 %copy-start.2 = (f32[128]{0:T(128)S(1)}, f32[128]{0:T(128)}, u32[]{:S(2)}) copy-start(f32[128]{0:T(128)} %param.13) | copy-start | bytes 1540
  10.1 8.9 %copy-start.3 = (f32[128]{0:T(128)S(1)}, f32[128]{0:T(128)}, u32[]{:S(2)}) copy-start(f32[128]{0:T(128)} %param.12) | copy-start | bytes 1540
  10.1 8.9 %copy-start.4 = (f32[128,4]{0,1:T(4,128)S(1)}, f32[128,4]{0,1:T(4,128)}, u32[]{:S(2)}) copy-start(f32[128,4]{0,1:T(4,128)} %param.16) | copy-start | bytes 6148
  16.9 34.9 %copy-start.6 = (s32[256]{0:T(256)S(1)}, s32[256]{0:T(256)}, u32[]{:S(2)}) copy-start(s32[256]{0:T(256)} %param.11) | copy-start | bytes 3076
  18.2 52.1 %all-gather.5.cloned.1.call-start = ((), (), s32[]{:S(2)}) async-start(), calls=%async_computation.2 | async-start | bytes 1572864 | tf_op jit(solution)/shard_map/all_gather | solution.py:41
  46.5 17.8 %all-to-all-start = ((f32[4,256,128]{2,0,1:T(4,128)}), f32[4,256,128]{2,0,1:T(4,128)S(1)}, u32[]{:S(2)}, u32[]{:S(2)}) async-start(f32[4,256,128]{2,0,1:T(4,128)} %all_gather.11), calls=%async_computation | async-start | bytes 1048576 | tf_op jit(solution)/shard_map/all_to_all | solution.py:38
  70.3 36.8 %copy-start.5 = (f32[128,128]{1,0:T(8,128)S(1)}, f32[128,128]{1,0:T(8,128)}, u32[]{:S(2)}) copy-start(f32[128,128]{1,0:T(8,128)} %param.17) | copy-start | bytes 196612
  70.3 36.8 %copy-start.7 = (f32[128]{0:T(128)S(1)}, f32[128]{0:T(128)}, u32[]{:S(2)}) copy-start(f32[128]{0:T(128)} %param.15) | copy-start | bytes 1540
Sparse Core Ops, SparseCore 0:
  18.3 23.9 all-gather.2
  43.9 26.3 all-gather.4
where the time goes:
time: 118 us; the launch traced here: 117 us
  blocking collectives  26 us (22%)
  matrix products  25.9 us (22%)
  local copies, waits for them, and re-layouts  20.5 us (17%)
  waiting for transfers between devices  18.3 us (16%)
  between operations  13.6 us (12%)
  other arithmetic  9.11 us (8%)
  starting transfers between devices  3.53 us (3%)
    all_gather x1, blocking collectives, body(): bias_cols = lax.all_gather(bias_local, 'row', axis=1, tiled=True)  26 us
    dynamic_slice x48, local copies, waits for them, and re-layouts, body(): lax.map(one_row, (query_half, key_all, value_all))  17.7 us
    all_to_all x1, waiting for transfers between devices, body(): lax.all_to_all(bias_cols, 'chan', split_axis=1, concat_axis=2, tiled=True)  12.5 us
    dot_general x16, matrix products, one_row(): return jnp.einsum('hjk,khd->jhd', weights, values, precision=highest)  8.53 us
    dot_general x1, matrix products, body(): jnp.einsum('rjc,ce->rje', normed, proj_weight, precision=highest)  6.75 us
    dot_general x16, matrix products, one_row(): jnp.einsum('jhd,khd->hjk', queries, key_heads, preferred_element_type=jnp...  5.72 us
    all_gather x1, waiting for transfers between devices, body(): lax.all_gather(key_half, 'chan', axis=1, tiled=True)  5.06 us
    reduce_sum x16, other arithmetic, one_row(): jax.nn.softmax(jnp.where(valid_keys[None, None, :], scores, -1000000000.0...  4.19 us
  transfers between devices with their start and end apart: 3, of which 2 were waited for; matrix products, arithmetic and copies ran while one was open for 3% of the time, Pallas kernels for 0%

commit v1 on v0

v1 whole, which is shorter than its diff:
```python
import functools
import math

import jax
import jax.numpy as jnp
from jax import lax
from jax.experimental import pallas as pl
from jax.experimental.pallas import tpu as pltpu
from jax.sharding import PartitionSpec as P

HEADS = 4
MESH = pl.DeviceIdType.MESH
NT = (((1,), (1,)), ((), ()))
NEVER = -1e30


def kernel(
    chans,
    group,
    x_ref,
    mask_ref,
    gain_ref,
    shift_ref,
    proj_ref,
    gate_ref,
    bw_ref,
    ow_ref,
    out_ref,
    xall,
    blocks,
    stage,
    own_bias,
    bias,
    w_own,
    w_kv,
    w_out,
    bw_pad,
    queries,
    gates,
    keys,
    values,
    result,
    x_send,
    x_recv,
    far_send,
    far_recv,
    near_send,
    near_recv,
    out_sem,
):
    rows, span, width = x_ref.shape
    total = chans * span
    head_dim = width // HEADS
    r = lax.axis_index("row")
    c = lax.axis_index("chan")
    hi = r // group
    lo = r % group
    is_home = (hi == c).astype(jnp.int32)

    barrier = pltpu.get_barrier_semaphore()
    for d in range(1, chans):
        pl.semaphore_signal(barrier, inc=1, device_id=(r, (c + d) % chans), device_id_type=MESH)
    for s in range(chans):

        @pl.when(jnp.logical_or(hi != c, c != s))
        def _():
            pl.semaphore_signal(barrier, inc=1, device_id=(c * group + lo, s), device_id_type=MESH)

    for d in range(1, group):
        pl.semaphore_signal(
            barrier, inc=1, device_id=(hi * group + (lo + d) % group, c), device_id_type=MESH
        )

    exp_scale = math.log2(math.e)
    proj = proj_ref[...]
    w_own[...] = proj.astype(jnp.bfloat16)
    w_kv[...] = proj[:, width : 3 * width].astype(jnp.bfloat16)
    w_out[...] = ow_ref[...].astype(jnp.bfloat16)
    bw_pad[...] = jnp.zeros_like(bw_pad)
    bw_pad[:, :HEADS] = bw_ref[...]
    bw_t = jnp.transpose(bw_pad[...])[:8].astype(jnp.bfloat16)
    gain = gain_ref[...].reshape(1, 1, width)
    shift = shift_ref[...].reshape(1, 1, width)

    step = 4 if rows % 4 == 0 else 1

    def norm_rows(n, carry):
        x = x_ref[pl.ds(n * step, step)]
        centered = x - jnp.mean(x, axis=-1, keepdims=True)
        variance = jnp.mean(centered * centered, axis=-1, keepdims=True)
        normed = (centered * lax.rsqrt(variance + 1e-05) * gain + shift).astype(jnp.bfloat16)
        for m in range(step):
            xall[n * step + m, c] = normed[m]
            local = lax.dot_general(bw_t, normed[m], NT, preferred_element_type=jnp.float32)
            stage[:, n * step + m, :] = local[:HEADS]
        return carry

    lax.fori_loop(0, rows // step, norm_rows, 0)
    own_bias[...] = stage[...].astype(jnp.bfloat16)

    @pl.when(hi == c)
    def _():
        blocks[lo, c] = stage[...].astype(jnp.bfloat16)

    pl.semaphore_wait(barrier, 2 * chans - 1 - is_home + group - 1)

    def far_copy(g, source):
        return pltpu.make_async_remote_copy(
            src_ref=own_bias,
            dst_ref=blocks.at[lo, source],
            send_sem=far_send.at[g],
            recv_sem=far_recv.at[source],
            device_id=(g * group + lo, hi),
            device_id_type=MESH,
        )

    for g in range(chans):

        @pl.when(jnp.logical_or(hi != c, hi != g))
        def _():
            far_copy(g, c).start()

    def x_copy(i, d, source):
        return pltpu.make_async_remote_copy(
            src_ref=xall.at[i, source],
            dst_ref=xall.at[i, source],
            send_sem=x_send.at[d - 1, i],
            recv_sem=x_recv.at[d - 1, i],
            device_id=(r, (c + d) % chans),
            device_id_type=MESH,
        )

    def send_row(i, carry):
        for d in range(1, chans):
            x_copy(i, d, c).start()
        return carry

    lax.fori_loop(0, rows, send_row, 0)

    scaling = exp_scale / math.sqrt(head_dim)

    def project_own(i, carry):
        full = jnp.dot(xall[i, c], w_own[...], preferred_element_type=jnp.float32)
        queries[i] = (full[:, :width] * scaling).astype(jnp.bfloat16)
        keys[i, c] = full[:, width : 2 * width].astype(jnp.bfloat16)
        values[i, c, :, :width] = full[:, 2 * width : 3 * width].astype(jnp.bfloat16)
        gates[i] = jax.nn.sigmoid(full[:, 3 * width :] + gate_ref[...])
        for s in range(chans):
            values[i, s, :, width:] = jnp.ones((span, width), jnp.bfloat16)
        return carry

    lax.fori_loop(0, rows, project_own, 0)

    for s in range(chans):

        @pl.when(jnp.logical_or(hi != c, c != s))
        def _():
            far_copy(s, s).wait_recv()

    def near_copy(d, source):
        return pltpu.make_async_remote_copy(
            src_ref=blocks.at[source],
            dst_ref=blocks.at[source],
            send_sem=near_send.at[d - 1],
            recv_sem=near_recv.at[d - 1],
            device_id=(hi * group + (lo + d) % group, c),
            device_id_type=MESH,
        )

    for d in range(1, group):
        near_copy(d, lo).start()
    for d in range(1, group):
        near_copy(d, (lo + group - d) % group).wait_recv()

    valid = mask_ref[...] > 0
    for s in range(chans):
        keep = valid[:, s * span : (s + 1) * span].reshape(1, 1, span)
        for h in range(HEADS):
            part = blocks[:, s, h].astype(jnp.float32) * exp_scale
            bias[h, :, :, s * span : (s + 1) * span] = jnp.where(keep, part, NEVER)

    lane = lax.broadcasted_iota(jnp.int32, (span, width), 1) // head_dim

    def out_copy(i):
        return pltpu.make_async_copy(result.at[i], out_ref.at[i], out_sem.at[i])

    def attend(i, carry):
        for d in range(1, chans):
            source = (c + chans - d) % chans
            x_copy(i, d, source).wait_recv()
            kv = jnp.dot(xall[i, source], w_kv[...], preferred_element_type=jnp.float32)
            keys[i, source] = kv[:, :width].astype(jnp.bfloat16)
            values[i, source, :, :width] = kv[:, width:].astype(jnp.bfloat16)
        query = queries[i]
        key = keys[i].reshape(total, width)
        value = values[i].reshape(total, 2 * width)
        top = jnp.zeros((span, width), jnp.float32)
        norm = jnp.zeros((span, width), jnp.float32)
        for h in range(HEADS):
            mine = jnp.where(lane == h, query, jnp.zeros_like(query))
            scores = lax.dot_general(mine, key, NT, preferred_element_type=jnp.float32)
            scores = scores + bias[h].reshape(span, total)
            peak = jnp.max(scores, axis=-1, keepdims=True)
            weights = jnp.exp2(scores - peak).astype(jnp.bfloat16)
            both = jnp.dot(weights, value, preferred_element_type=jnp.float32)
            top = jnp.where(lane == h, both[:, :width], top)
            norm = jnp.where(lane == h, both[:, width:], norm)
        gated = gates[i] * (top / norm)
        result[i] = jnp.dot(
            gated.astype(jnp.bfloat16), w_out[...], preferred_element_type=jnp.float32
        )
        out_copy(i).start()
        return carry

    lax.fori_loop(0, rows, attend, 0)

    for g in range(chans):

        @pl.when(jnp.logical_or(hi != c, hi != g))
        def _():
            far_copy(g, c).wait_send()

    for d in range(1, group):
        near_copy(d, lo).wait_send()

    def finish(i, carry):
        for d in range(1, chans):
            x_copy(i, d, c).wait_send()
        out_copy(i).wait()
        return carry

    lax.fori_loop(0, rows, finish, 0)


def body(
    chans,
    pair_rep,
    residue_mask,
    norm_gain,
    norm_shift,
    proj_weight,
    gate_shift,
    bias_weight,
    out_weight,
):
    rows, span, width = pair_rep.shape
    group = span // rows
    total = chans * span
    vmem = pl.BlockSpec(memory_space=pltpu.VMEM)
    half = jnp.bfloat16
    full = jnp.float32
    return pl.pallas_call(
        functools.partial(kernel, chans, group),
        out_shape=jax.ShapeDtypeStruct((rows, span, width), full),
        in_specs=[vmem] * 8,
        out_specs=pl.BlockSpec(memory_space=pl.ANY),
        scratch_shapes=[
            pltpu.VMEM((rows, chans, span, width), half),
            pltpu.VMEM((group, chans, HEADS, rows, span), half),
            pltpu.VMEM((HEADS, rows, span), full),
            pltpu.VMEM((HEADS, rows, span), half),
            pltpu.VMEM((HEADS, group, rows, total), full),
            pltpu.VMEM((width, 4 * width), half),
            pltpu.VMEM((width, 2 * width), half),
            pltpu.VMEM((width, width), half),
            pltpu.VMEM((width, width), full),
            pltpu.VMEM((rows, span, width), half),
            pltpu.VMEM((rows, span, width), full),
            pltpu.VMEM((rows, chans, span, width), half),
            pltpu.VMEM((rows, chans, span, 2 * width), half),
            pltpu.VMEM((rows, span, width), full),
            pltpu.SemaphoreType.DMA((chans - 1, rows)),
            pltpu.SemaphoreType.DMA((chans - 1, rows)),
            pltpu.SemaphoreType.DMA((chans,)),
            pltpu.SemaphoreType.DMA((chans,)),
            pltpu.SemaphoreType.DMA((group - 1,)),
            pltpu.SemaphoreType.DMA((group - 1,)),
            pltpu.SemaphoreType.DMA((rows,)),
        ],
        compiler_params=pltpu.CompilerParams(
            collective_id=0, has_side_effects=True, vmem_limit_bytes=56 * 1024 * 1024
        ),
    )(
        pair_rep,
        residue_mask.reshape(1, total),
        norm_gain.reshape(1, width),
        norm_shift.reshape(1, width),
        proj_weight,
        gate_shift.reshape(1, width),
        bias_weight,
        out_weight,
    )


def solution(mesh):
    return jax.shard_map(
        functools.partial(body, mesh.shape["chan"]),
        mesh=mesh,
        in_specs=(P("row", "chan", None), P(), P(), P(), P(), P(), P(), P()),
        out_specs=P("row", "chan", None),
        check_vma=False,
    )
```

time: 118 us -> 30.8 us (0.26)
  Pallas kernels: 0 us -> 26.9 us
  blocking collectives: 26 us -> 0 us
  matrix products: 25.9 us -> 0 us
  waiting for transfers between devices: 18.3 us -> 0 us
  local copies, waits for them, and re-layouts: 20.5 us -> 3.72 us
  between operations: 13.6 us -> 0.01 us
  other arithmetic: 9.11 us -> 0 us
  starting transfers between devices: 3.53 us -> 0 us
    pallas_call x0 -> x1, Pallas kernels: none -> 26.9 us  [body(): pl.pallas_call(functools.partial(kernel, chans, group), out_shape=jax.Sha...]
    all_gather x1 -> x0, blocking collectives: 26 us -> none  [body(): bias_cols = lax.all_gather(bias_local, 'row', axis=1, tiled=True)]
    dot_general x35 -> x0, matrix products: 25.9 us -> none  [the longest x16 8.53 us: one_row(): return jnp.einsum('hjk,khd->jhd', weights, values, precision=highest)]
    dynamic_slice x48 -> x0, local copies, waits for them, and re-layouts: 17.7 us -> none  [body(): lax.map(one_row, (query_half, key_all, value_all))]
    all_to_all x1 -> x0, waiting for transfers between devices: 12.5 us -> none  [body(): lax.all_to_all(bias_cols, 'chan', split_axis=1, concat_axis=2, tiled=True)]
    reduce_sum x18 -> x0, other arithmetic: 7.65 us -> none  [the longest x16 4.19 us: one_row(): jax.nn.softmax(jnp.where(valid_keys[None, None, :], scores, -1000000000.0...]
    all_gather x2 -> x0, waiting for transfers between devices: 5.08 us -> none  [the longest x1 5.06 us: body(): lax.all_gather(key_half, 'chan', axis=1, tiled=True)]
    unnamed x16 -> x4, local copies, waits for them, and re-layouts: 0.04 us -> 3.72 us
  transfers between devices with their start and end apart: 3 -> 0, of which waited for: 2 -> 0; matrix products, arithmetic and copies ran while one was open for 3% -> 0% of each run, Pallas kernels for 0% -> 0%
where the time goes in v1:
time: 30.8 us; the launch traced here: 30.6 us
  Pallas kernels  26.9 us (87%)
  local copies, waits for them, and re-layouts  3.72 us (12%)
    pallas_call x1, Pallas kernels, body(): pl.pallas_call(functools.partial(kernel, chans, group), out_shape=jax.Sha...  26.9 us
    unnamed x4, local copies, waits for them, and re-layouts  3.72 us

profile of v1, /device:TPU:0, one launch (start us, length us, event | category | flops | bytes accessed | tf_op | source)
XLA Modules:
  0.0 30.6 jit_solution(3965491879612102235)
XLA Ops:
  0.0 0.0 copy-start
  0.0 0.7 %copy-done = f32[128,4]{0,1:T(4,128)S(1)} copy-done((f32[128,4]{0,1:T(4,128)S(1)}, f32[128,4]{0,1:T(4,128)}, u32[]{:S(2)}) %copy-start) | copy-done | bytes 2072
  0.7 0.7 %copy.9.bw_ref = f32[128,4]{1,0:T(8,128)} copy(f32[128,4]{0,1:T(4,128)S(1)} %copy-done) | data formatting | bytes 4096 | tf_op args[6]
  1.4 26.9 %shard_map.82 = f32[16,128,128]{2,1,0:T(8,128)} custom-call(f32[16,128,128]{2,1,0:T(8,128)} %x_ref.1, s32[1,256]{1,0:T(1,128)} %bitcast.4, f32[1,128]{1,0:T(1,128)} %bitcast.5, f32[1,128]{1,0:T(1,128)} %bitcast.6, f32[128,512]{1,0:T(8,128)} %proj_ref.1, f32[1,128]{1,0:T(1,128)} %bitcast.7, f32[128,4]{1,0:T(8,128)} %copy.9.bw_ref, f32[128,128]{1,0:T(8,128)} %ow_ref.1), custom_call_target="tpu_custom_call" | custom-call | tf_op jit(solution)/shard_map/pallas_call | solution.py:252
  28.3 2.3 %copy.11 = f32[16,128,128]{2,1,0:T(8,128)} copy(f32[16,128,128]{2,1,0:T(8,128)} %shard_map.82) | data formatting | bytes 2097152
Async XLA Ops:
  0.0 0.7 %copy-start = (f32[128,4]{0,1:T(4,128)S(1)}, f32[128,4]{0,1:T(4,128)}, u32[]{:S(2)}) copy-start(f32[128,4]{0,1:T(4,128)} %param.14) | copy-start | bytes 6148

commit v2 on v1

--- a/solution.py
+++ b/solution.py
@@ -12,6 +12,11 @@
 MESH = pl.DeviceIdType.MESH
 NT = (((1,), (1,)), ((), ()))
 NEVER = -1e30
+
+
+def halves(value):
+    high = value.astype(jnp.bfloat16)
+    return high, (value - high.astype(jnp.float32)).astype(jnp.bfloat16)
 
 
 def kernel(
@@ -34,7 +39,7 @@
     w_own,
     w_kv,
     w_out,
-    bw_pad,
+    xlow,
     queries,
     gates,
     keys,
@@ -72,13 +77,18 @@
         )
 
     exp_scale = math.log2(math.e)
-    proj = proj_ref[...]
-    w_own[...] = proj.astype(jnp.bfloat16)
-    w_kv[...] = proj[:, width : 3 * width].astype(jnp.bfloat16)
-    w_out[...] = ow_ref[...].astype(jnp.bfloat16)
-    bw_pad[...] = jnp.zeros_like(bw_pad)
-    bw_pad[:, :HEADS] = bw_ref[...]
-    bw_t = jnp.transpose(bw_pad[...])[:8].astype(jnp.bfloat16)
+    proj_high, proj_low = halves(proj_ref[...])
+    w_own[:width] = proj_high
+    w_own[width : 2 * width] = proj_high
+    w_own[2 * width :] = proj_low
+    w_kv[:width] = proj_high[:, width : 3 * width]
+    w_kv[width:] = proj_low[:, width : 3 * width]
+    out_high, out_low = halves(ow_ref[...])
+    w_out[:width] = out_high
+    w_out[width : 2 * width] = out_high
+    w_out[2 * width :] = out_low
+    bw_high, bw_low = halves(bw_ref[...])
+    bw_t = jnp.concatenate([bw_high, bw_high, bw_low], axis=1)
     gain = gain_ref[...].reshape(1, 1, width)
     shift = shift_ref[...].reshape(1, 1, width)
 
@@ -88,11 +98,17 @@
         x = x_ref[pl.ds(n * step, step)]
         centered = x - jnp.mean(x, axis=-1, keepdims=True)
         variance = jnp.mean(centered * centered, axis=-1, keepdims=True)
-        normed = (centered * lax.rsqrt(variance + 1e-05) * gain + shift).astype(jnp.bfloat16)
+        high, low = halves(centered * lax.rsqrt(variance + 1e-05) * gain + shift)
         for m in range(step):
-            xall[n * step + m, c] = normed[m]
-            local = lax.dot_general(bw_t, normed[m], NT, preferred_element_type=jnp.float32)
-            stage[:, n * step + m, :] = local[:HEADS]
+            xall[n * step + m, c] = high[m]
+            xlow[n * step + m] = low[m]
+            local = lax.dot_general(
+                bw_t,
+                jnp.concatenate([high[m], low[m], high[m]], axis=1),
+                NT,
+                preferred_element_type=jnp.float32,
+            )
+            stage[:, n * step + m, :] = local[:HEADS] * exp_scale
         return carry
 
     lax.fori_loop(0, rows // step, norm_rows, 0)
@@ -140,7 +156,12 @@
     scaling = exp_scale / math.sqrt(head_dim)
 
     def project_own(i, carry):
-        full = jnp.dot(xall[i, c], w_own[...], preferred_element_type=jnp.float32)
+        high = xall[i, c]
+        full = jnp.dot(
+            jnp.concatenate([high, xlow[i], high], axis=1),
+            w_own[...],
+            preferred_element_type=jnp.float32,
+        )
         queries[i] = (full[:, :width] * scaling).astype(jnp.bfloat16)
         keys[i, c] = full[:, width : 2 * width].astype(jnp.bfloat16)
         values[i, c, :, :width] = full[:, 2 * width : 3 * width].astype(jnp.bfloat16)
@@ -169,6 +190,24 @@
 
     for d in range(1, group):
         near_copy(d, lo).start()
+
+    def project_other(i, carry):
+        for d in range(1, chans):
+            source = (c + chans - d) % chans
+            x_copy(i, d, source).wait_recv()
+            other = xall[i, source]
+            kv = jnp.dot(
+                jnp.concatenate([other, other], axis=1),
+                w_kv[...],
+                preferred_element_type=jnp.float32,
+            )
+            keys[i, source] = kv[:, :width].astype(jnp.bfloat16)
+            values[i, source, :, :width] = kv[:, width:].astype(jnp.bfloat16)
+        return carry
+
+    early = rows // 2
+    lax.fori_loop(0, early, project_other, 0)
+
     for d in range(1, group):
         near_copy(d, (lo + group - d) % group).wait_recv()
 
@@ -176,7 +215,7 @@
     for s in range(chans):
         keep = valid[:, s * span : (s + 1) * span].reshape(1, 1, span)
         for h in range(HEADS):
-            part = blocks[:, s, h].astype(jnp.float32) * exp_scale
+            part = blocks[:, s, h].astype(jnp.float32)
             bias[h, :, :, s * span : (s + 1) * span] = jnp.where(keep, part, NEVER)
 
     lane = lax.broadcasted_iota(jnp.int32, (span, width), 1) // head_dim
@@ -185,12 +224,6 @@
         return pltpu.make_async_copy(result.at[i], out_ref.at[i], out_sem.at[i])
 
     def attend(i, carry):
-        for d in range(1, chans):
-            source = (c + chans - d) % chans
-            x_copy(i, d, source).wait_recv()
-            kv = jnp.dot(xall[i, source], w_kv[...], preferred_element_type=jnp.float32)
-            keys[i, source] = kv[:, :width].astype(jnp.bfloat16)
-            values[i, source, :, :width] = kv[:, width:].astype(jnp.bfloat16)
         query = queries[i]
         key = keys[i].reshape(total, width)
         value = values[i].reshape(total, 2 * width)
@@ -205,14 +238,21 @@
             both = jnp.dot(weights, value, preferred_element_type=jnp.float32)
             top = jnp.where(lane == h, both[:, :width], top)
             norm = jnp.where(lane == h, both[:, width:], norm)
-        gated = gates[i] * (top / norm)
+        high, low = halves(gates[i] * (top / norm))
         result[i] = jnp.dot(
-            gated.astype(jnp.bfloat16), w_out[...], preferred_element_type=jnp.float32
+            jnp.concatenate([high, low, high], axis=1),
+            w_out[...],
+            preferred_element_type=jnp.float32,
         )
         out_copy(i).start()
         return carry
 
-    lax.fori_loop(0, rows, attend, 0)
+    def attend_ahead(i, carry):
+        project_other(i + early, carry)
+        return attend(i, carry)
+
+    lax.fori_loop(0, rows - early, attend_ahead, 0)
+    lax.fori_loop(rows - early, rows, attend, 0)
 
     for g in range(chans):
 
@@ -260,10 +300,10 @@
             pltpu.VMEM((HEADS, rows, span), full),
             pltpu.VMEM((HEADS, rows, span), half),
             pltpu.VMEM((HEADS, group, rows, total), full),
-            pltpu.VMEM((width, 4 * width), half),
-            pltpu.VMEM((width, 2 * width), half),
-            pltpu.VMEM((width, width), half),
-            pltpu.VMEM((width, width), full),
+            pltpu.VMEM((3 * width, 4 * width), half),
+            pltpu.VMEM((2 * width, 2 * width), half),
+            pltpu.VMEM((3 * width, width), half),
+            pltpu.VMEM((rows, span, width), half),
             pltpu.VMEM((rows, span, width), half),
             pltpu.VMEM((rows, span, width), full),
             pltpu.VMEM((rows, chans, span, width), half),
@@ -287,7 +327,7 @@
         norm_shift.reshape(1, width),
         proj_weight,
         gate_shift.reshape(1, width),
-        bias_weight,
+        bias_weight.T,
         out_weight,
     )
 

time: 30.8 us -> 30.3 us (0.984)
  local copies, waits for them, and re-layouts: 3.72 us -> 2.3 us
  Pallas kernels: 26.9 us -> 27.8 us
    unnamed x4 -> x1, local copies, waits for them, and re-layouts: 3.72 us -> 2.3 us
    pallas_call x1, Pallas kernels: 26.9 us -> 27.8 us  [body(): pl.pallas_call(functools.partial(kernel, chans, group), out_shape=jax.Sha...]
where the time goes in v2:
time: 30.3 us; the launch traced here: 30.1 us
  Pallas kernels  27.8 us (92%)
  local copies, waits for them, and re-layouts  2.3 us (8%)
    pallas_call x1, Pallas kernels, body(): pl.pallas_call(functools.partial(kernel, chans, group), out_shape=jax.Sha...  27.8 us
    unnamed x1, local copies, waits for them, and re-layouts  2.3 us

profile of v2, /device:TPU:0, one launch (start us, length us, event | category | flops | bytes accessed | tf_op | source)
XLA Modules:
  0.0 30.1 jit_solution(4952404446692831762)
XLA Ops:
  0.0 27.8 %shard_map.82 = f32[16,128,128]{2,1,0:T(8,128)} custom-call(f32[16,128,128]{2,1,0:T(8,128)} %x_ref.1, s32[1,256]{1,0:T(1,128)} %bitcast.6, f32[1,128]{1,0:T(1,128)} %bitcast.7, f32[1,128]{1,0:T(1,128)} %bitcast.8, f32[128,512]{1,0:T(8,128)} %proj_ref.1, f32[1,128]{1,0:T(1,128)} %bitcast.9, f32[4,128]{1,0:T(4,128)} %bitcast.5, f32[128,128]{1,0:T(8,128)} %ow_ref.1), custom_call_target="tpu_custom_call" | custom-call | tf_op jit(solution)/shard_map/pallas_call | solution.py:292
  27.9 2.3 %copy.10 = f32[16,128,128]{2,1,0:T(8,128)} copy(f32[16,128,128]{2,1,0:T(8,128)} %shard_map.82) | data formatting | bytes 2097152

commit v3 on v2

--- a/solution.py
+++ b/solution.py
@@ -151,7 +151,8 @@
             x_copy(i, d, c).start()
         return carry
 
-    lax.fori_loop(0, rows, send_row, 0)
+    early = rows // 4
+    lax.fori_loop(0, early, send_row, 0)
 
     scaling = exp_scale / math.sqrt(head_dim)
 
@@ -190,6 +191,7 @@
 
     for d in range(1, group):
         near_copy(d, lo).start()
+    lax.fori_loop(early, rows, send_row, 0)
 
     def project_other(i, carry):
         for d in range(1, chans):
@@ -205,7 +207,6 @@
             values[i, source, :, :width] = kv[:, width:].astype(jnp.bfloat16)
         return carry
 
-    early = rows // 2
     lax.fori_loop(0, early, project_other, 0)
 
     for d in range(1, group):

time: 30.3 us -> 30 us (0.990)
    pallas_call x1, Pallas kernels: 27.8 us -> 27.5 us  [body(): pl.pallas_call(functools.partial(kernel, chans, group), out_shape=jax.Sha...]
where the time goes in v3:
time: 30 us; the launch traced here: 29.8 us
  Pallas kernels  27.5 us (92%)
  local copies, waits for them, and re-layouts  2.3 us (8%)
    pallas_call x1, Pallas kernels, body(): pl.pallas_call(functools.partial(kernel, chans, group), out_shape=jax.Sha...  27.5 us
    unnamed x1, local copies, waits for them, and re-layouts  2.3 us

profile of v3, /device:TPU:0, one launch (start us, length us, event | category | flops | bytes accessed | tf_op | source)
XLA Modules:
  0.0 29.8 jit_solution(4958884700149232248)
XLA Ops:
  0.0 27.5 %shard_map.82 = f32[16,128,128]{2,1,0:T(8,128)} custom-call(f32[16,128,128]{2,1,0:T(8,128)} %x_ref.1, s32[1,256]{1,0:T(1,128)} %bitcast.6, f32[1,128]{1,0:T(1,128)} %bitcast.7, f32[1,128]{1,0:T(1,128)} %bitcast.8, f32[128,512]{1,0:T(8,128)} %proj_ref.1, f32[1,128]{1,0:T(1,128)} %bitcast.9, f32[4,128]{1,0:T(4,128)} %bitcast.5, f32[128,128]{1,0:T(8,128)} %ow_ref.1), custom_call_target="tpu_custom_call" | custom-call | tf_op jit(solution)/shard_map/pallas_call | solution.py:293
  27.5 2.3 %copy.10 = f32[16,128,128]{2,1,0:T(8,128)} copy(f32[16,128,128]{2,1,0:T(8,128)} %shard_map.82) | data formatting | bytes 2097152

commit v4 on v2

--- a/solution.py
+++ b/solution.py
@@ -205,7 +205,7 @@
             values[i, source, :, :width] = kv[:, width:].astype(jnp.bfloat16)
         return carry
 
-    early = rows // 2
+    early = rows // 8
     lax.fori_loop(0, early, project_other, 0)
 
     for d in range(1, group):

time: 30.3 us -> 30.4 us (level)
  no operation moved by 1% of the time
where the time goes in v4:
time: 30.4 us; the launch traced here: 30.2 us
  Pallas kernels  27.9 us (92%)
  local copies, waits for them, and re-layouts  2.3 us (8%)
    pallas_call x1, Pallas kernels, body(): pl.pallas_call(functools.partial(kernel, chans, group), out_shape=jax.Sha...  27.9 us
    unnamed x1, local copies, waits for them, and re-layouts  2.3 us

profile of v4, /device:TPU:0, one launch (start us, length us, event | category | flops | bytes accessed | tf_op | source)
XLA Modules:
  0.0 30.2 jit_solution(15322659539409518019)
XLA Ops:
  0.0 27.9 %shard_map.82 = f32[16,128,128]{2,1,0:T(8,128)} custom-call(f32[16,128,128]{2,1,0:T(8,128)} %x_ref.1, s32[1,256]{1,0:T(1,128)} %bitcast.6, f32[1,128]{1,0:T(1,128)} %bitcast.7, f32[1,128]{1,0:T(1,128)} %bitcast.8, f32[128,512]{1,0:T(8,128)} %proj_ref.1, f32[1,128]{1,0:T(1,128)} %bitcast.9, f32[4,128]{1,0:T(4,128)} %bitcast.5, f32[128,128]{1,0:T(8,128)} %ow_ref.1), custom_call_target="tpu_custom_call" | custom-call | tf_op jit(solution)/shard_map/pallas_call | solution.py:292
  27.9 2.3 %copy.10 = f32[16,128,128]{2,1,0:T(8,128)} copy(f32[16,128,128]{2,1,0:T(8,128)} %shard_map.82) | data formatting | bytes 2097152
